TPU v7x, 32 devices: a whole 2x2x4 slice. The times are simulated.
32 devices in a mesh: fsdp: 4 (over z), ep: 8 (over y, x, core).
Axes of the slice: x: 2, y: 2, z: 4, core: 2. Of those that a mesh axis runs over, the one named last changes fastest.
Arguments:
- grad_out: bfloat16 [4096, 768], P(('fsdp', 'ep'))
- expert_idx: int32 [4096, 1], P(('fsdp', 'ep'))
- slot_pos: int32 [4096, 1], P(('fsdp', 'ep'))
- gates: float32 [4096, 1], P(('fsdp', 'ep'))
- x_disp: bfloat16 [32, 256, 768], P('ep', 'fsdp')
- h_gate: bfloat16 [32, 256, 3072], P('ep', 'fsdp')
- h_up: bfloat16 [32, 256, 3072], P('ep', 'fsdp')
- y_disp: bfloat16 [32, 256, 768], P('ep', 'fsdp')
- w_gate: bfloat16 [32, 768, 3072], P('ep', 'fsdp')
- w_down: bfloat16 [32, 3072, 768], P('ep', 'fsdp')
- w_up: bfloat16 [32, 768, 3072], P('ep', 'fsdp')
Outputs:
- output 1: bfloat16 [4096, 768], P(('fsdp', 'ep'))
- output 2: float32 [4096, 1], P(('fsdp', 'ep'))
- output 3: float32 [32, 768, 3072], P('ep', 'fsdp')
- output 4: float32 [32, 3072, 768], P('ep', 'fsdp')
- output 5: float32 [32, 768, 3072], P('ep', 'fsdp')
All inputs are finite; a program needn't handle non-finite values.
Results may differ from a plain program's by a relative error of at most 0.001.
Values are sent between devices in bfloat16 or wider.
A program may use at most 1 GiB of HBM per device.

v0:
```python
import jax
import jax.numpy as jnp
from jax import lax
from jax.sharding import PartitionSpec as P


def expert_grads(dy_rows, gate_rows, x_rows, h_gate, h_up, y_rows, w_gate, w_down, w_up):
    g_rows = (dy_rows.astype(jnp.float32) * gate_rows[..., None]).astype(jnp.bfloat16)
    gate_pre = h_gate.astype(jnp.float32)
    up_pre = h_up.astype(jnp.float32)
    sigmoid_gate = jax.nn.sigmoid(gate_pre)
    silu_gate = gate_pre * sigmoid_gate
    act_rows = (silu_gate * up_pre).astype(jnp.bfloat16)
    d_act = jnp.einsum('erd,efd->erf', g_rows, w_down, preferred_element_type=jnp.float32)
    dh_gate = (d_act * up_pre * sigmoid_gate * (1.0 + gate_pre * (1.0 - sigmoid_gate))).astype(jnp.bfloat16)
    dh_up = (d_act * silu_gate).astype(jnp.bfloat16)
    dx_rows = (jnp.einsum('erf,edf->erd', dh_gate, w_gate, preferred_element_type=jnp.float32) + jnp.einsum('erf,edf->erd', dh_up, w_up, preferred_element_type=jnp.float32)).astype(jnp.bfloat16)
    dgate_rows = jnp.einsum('erd,erd->er', dy_rows, y_rows, preferred_element_type=jnp.float32)
    dw_gate = jnp.einsum('erd,erf->edf', x_rows, dh_gate, preferred_element_type=jnp.float32)
    dw_down = jnp.einsum('erf,erd->efd', act_rows, g_rows, preferred_element_type=jnp.float32)
    dw_up = jnp.einsum('erd,erf->edf', x_rows, dh_up, preferred_element_type=jnp.float32)
    return dx_rows, dgate_rows, dw_gate, dw_down, dw_up


def solution(mesh):
    ep_n = mesh.shape['ep']
    tok_spec = P(('fsdp', 'ep'), None)
    row_spec = P('ep', 'fsdp', None)

    def local_backward(grad_out, expert_idx, slot_pos, gates, x_disp, h_gate, h_up, y_disp, w_gate, w_down, w_up):
        tok_n, top_n = expert_idx.shape
        e_loc, rows_loc, width = x_disp.shape
        slot_cap = rows_loc // ep_n
        slots_n = e_loc * ep_n * slot_cap
        choices = tok_n * top_n
        send_row = jnp.where(slot_pos >= 0, ((expert_idx % e_loc) * ep_n + expert_idx // e_loc) * slot_cap + slot_pos, slots_n).reshape(-1)
        src_choice = jnp.full((slots_n,), choices, jnp.int32).at[send_row].set(jnp.arange(choices, dtype=jnp.int32), mode='drop')
        send_dy = jnp.take(grad_out, src_choice // top_n, axis=0, mode='fill', fill_value=0).reshape(e_loc, ep_n, slot_cap, width)
        send_gate = jnp.take(gates.reshape(-1), src_choice, mode='fill', fill_value=0).reshape(e_loc, ep_n, slot_cap)
        recv_dy = lax.all_to_all(send_dy, 'ep', 1, 1, tiled=True).reshape(e_loc, rows_loc, width)
        recv_gate = lax.all_to_all(send_gate, 'ep', 1, 1, tiled=True).reshape(e_loc, rows_loc)
        full_w_gate = lax.all_gather(w_gate, 'fsdp', axis=1, tiled=True)
        full_w_down = lax.all_gather(w_down, 'fsdp', axis=1, tiled=True)
        full_w_up = lax.all_gather(w_up, 'fsdp', axis=1, tiled=True)
        dx_rows, dgate_rows, dw_gate, dw_down, dw_up = expert_grads(recv_dy, recv_gate, x_disp, h_gate, h_up, y_disp, full_w_gate, full_w_down, full_w_up)
        back_dx = lax.all_to_all(dx_rows.reshape(e_loc, ep_n, slot_cap, width), 'ep', 1, 1, tiled=True).reshape(slots_n, width)
        back_gate = lax.all_to_all(dgate_rows.reshape(e_loc, ep_n, slot_cap), 'ep', 1, 1, tiled=True).reshape(slots_n)
        picked = jnp.take(back_dx, send_row, axis=0, mode='fill', fill_value=0).reshape(tok_n, top_n, width)
        grad_x = jnp.sum(picked.astype(jnp.float32), axis=1).astype(jnp.bfloat16)
        grad_gates = jnp.take(back_gate, send_row, mode='fill', fill_value=0).reshape(tok_n, top_n)
        grad_w_gate = lax.psum_scatter(dw_gate, 'fsdp', scatter_dimension=1, tiled=True)
        grad_w_down = lax.psum_scatter(dw_down, 'fsdp', scatter_dimension=1, tiled=True)
        grad_w_up = lax.psum_scatter(dw_up, 'fsdp', scatter_dimension=1, tiled=True)
        return grad_x, grad_gates, grad_w_gate, grad_w_down, grad_w_up

    return jax.shard_map(local_backward, mesh=mesh, in_specs=(tok_spec, tok_spec, tok_spec, tok_spec, row_spec, row_spec, row_spec, row_spec, row_spec, row_spec, row_spec), out_specs=(tok_spec, tok_spec, row_spec, row_spec, row_spec), check_vma=False)
```

profile of v0, /device:TPU:0, one launch (start us, length us, event | category | flops | bytes accessed | tf_op | source)
XLA Modules:
  0.0 4080.0 jit_solution(13294275895771650536)
XLA Ops:
  7.2 0.0 copy-start
  7.2 0.0 all-gather.4.cloned.1.call-start
  7.2 0.7 all-gather.4.cloned.1.call-update
  7.9 0.0 all-gather.6.cloned.1.call-start
  8.0 0.7 all-gather.6.cloned.1.call-update
  8.7 0.0 all-gather.8.cloned.1.call-start
  8.8 0.7 all-gather.8.cloned.1.call-update
  9.5 1.0 scatter_custom_fusion
  10.5 0.1 broadcast_in_dim.50
  10.6 0.0 copy-done.2
  10.6 0.0 copy-start.4
  10.6 1.9 gather_fusion.1
  12.5 0.1 gather.25
  12.6 0.6 copy.30
  13.2 5.2 all-to-all-start.1
  18.5 0.0 copy-done.3
  18.5 1.2 gather_fusion
  19.7 0.9 copy_select_fusion
  20.5 2.5 all-to-all-done.1
  23.0 3.5 all-to-all-start
  26.5 0.0 all-reduce.7.cloned.1.call-start
  26.5 0.1 mul.39
  26.6 7.9 all-to-all-done
  34.5 300.5 %all-gather.4.cloned.1.call-done = bf16[4,3072,768]{2,1,0:T(8,128)(2,1)} async-done(((bf16[4,768,768]{2,1,0:T(8,128)(2,1)}), bf16[4,3072,768]{2,1,0:T(8,128)(2,1)}) %all-gather.4.cloned.1.call-update) | async-done | bytes 18874384 | tf_op jit(solution)/shard_map/all_gather | solution.py:43
  335.0 10.8 fusion.2
  345.8 1.7 copy-done.5
  347.5 14.7 convolution_bitcast_fusion
  362.2 44.6 %copy.37 = f32[4,768,3072]{2,0,1:T(4,128)} copy(f32[4,768,3072]{1,2,0:T(8,128)} %convolution_bitcast_fusion) | data formatting | bytes 75497472 | tf_op jit(solution)/shard_map/erd,erf->edf/dot_general | solution.py:21
  406.8 0.0 all-reduce.7.cloned.1.call-update
  406.8 0.0 all-reduce.5.cloned.1.call-start
  406.9 15.4 convolution_bitcast_fusion.1
  422.2 44.6 %copy.36 = f32[4,768,3072]{2,0,1:T(4,128)} copy(f32[4,768,3072]{1,2,0:T(8,128)} %convolution_bitcast_fusion.1) | data formatting | bytes 75497472 | tf_op jit(solution)/shard_map/erd,erf->edf/dot_general | solution.py:19
  466.8 0.0 all-reduce.5.cloned.1.call-update
  466.9 0.0 reduce-scatter.2.cloned.1.call-start
  466.9 15.6 fusion.8
  482.5 0.0 reduce-scatter.2.cloned.1.call-update
  482.5 1.0 copy-done.6
  483.5 0.2 fusion.13
  483.7 0.1 reshape.70
  483.8 0.6 copy.34
  484.4 3.7 all-to-all-start.3
  488.0 169.9 %all-gather.6.cloned.1.call-done = bf16[4,768,3072]{2,1,0:T(8,128)(2,1)} async-done(((bf16[4,192,3072]{2,1,0:T(8,128)(2,1)}), bf16[4,768,3072]{2,1,0:T(8,128)(2,1)}) %all-gather.6.cloned.1.call-update) | async-done | bytes 18874384 | tf_op jit(solution)/shard_map/all_gather | solution.py:42
  657.9 12.7 fusion.23
  670.6 0.0 copy-start.9
  670.6 310.2 %all-gather.8.cloned.1.call-done = bf16[4,768,3072]{2,1,0:T(8,128)(2,1)} async-done(((bf16[4,192,3072]{2,1,0:T(8,128)(2,1)}), bf16[4,768,3072]{2,1,0:T(8,128)(2,1)}) %all-gather.8.cloned.1.call-update) | async-done | bytes 18874384 | tf_op jit(solution)/shard_map/all_gather | solution.py:44
  980.8 10.8 fusion.11
  991.7 0.8 copy.32
  992.5 0.0 all-to-all-done.3
  992.5 3.7 all-to-all-start.2
  996.1 0.0 copy-done.9
  996.1 0.6 dynamic-slice
  997.4 0.1 reshape.71
  997.5 1.5 gather_fusion.3
  999.0 0.5 bitcast_select_fusion
  999.5 4.7 all-to-all-done.2
  1004.3 0.9 gather_fusion.2
  1005.1 0.8 broadcast_select_fusion
  1005.9 1211.9 %all-reduce.7.cloned.1.call-done = f32[4,768,3072]{2,0,1:T(4,128)} async-done(((f32[4,768,3072]{2,0,1:T(4,128)}), f32[4,768,3072]{2,0,1:T(4,128)}) %all-reduce.7.cloned.1.call-update) | async-done | bytes 37748752
  2217.8 9.4 constant_dynamic-slice_fusion
  2227.3 12.9 copy.39
  2240.1 1214.9 %all-reduce.5.cloned.1.call-done = f32[4,768,3072]{2,0,1:T(4,128)} async-done(((f32[4,768,3072]{2,0,1:T(4,128)}), f32[4,768,3072]{2,0,1:T(4,128)}) %all-reduce.5.cloned.1.call-update) | async-done | bytes 37748752
  3455.1 9.4 constant_dynamic-slice_fusion.1
  3464.4 13.2 copy.38
  3477.6 595.5 %reduce-scatter.2.cloned.1.call-done = f32[4,768,768]{2,1,0:T(8,128)} async-done(((f32[4,3072,768]{2,1,0:T(8,128)}), f32[4,768,768]{2,1,0:T(8,128)}) %reduce-scatter.2.cloned.1.call-update) | async-done | bytes 9437200 | tf_op jit(solution)/shard_map/reduce_scatter | solution.py:52
  (23 shorter events, 0.1 us)
Async XLA Ops:
  7.2 340.3 %copy-start = (bf16[4,64,768]{2,1,0:T(8,128)(2,1)S(1)}, bf16[4,64,768]{2,1,0:T(8,128)(2,1)}, u32[]{:S(2)}) copy-start(bf16[4,64,768]{2,1,0:T(8,128)(2,1)} %param.15) | copy-start | bytes 1179652
  7.2 327.9 %all-gather.4.cloned.1.call-start = ((), (), s32[]{:S(2)}) async-start(), calls=%async_computation.5 | async-start | bytes 23592960 | tf_op jit(solution)/shard_map/all_gather | solution.py:43
  7.9 650.0 %all-gather.6.cloned.1.call-start = ((), (), s32[]{:S(2)}) async-start(), calls=%async_computation.6 | async-start | bytes 23592960 | tf_op jit(solution)/shard_map/all_gather | solution.py:42
  8.7 0.8 copy-start.7
  8.7 0.8 copy-start.8
  8.7 1.9 copy-start.2
  8.7 9.8 copy-start.3
  8.7 972.1 %all-gather.8.cloned.1.call-start = ((), (), s32[]{:S(2)}) async-start(), calls=%async_computation.7 | async-start | bytes 23592960 | tf_op jit(solution)/shard_map/all_gather | solution.py:44
  10.6 324.4 %copy-start.4 = (bf16[4,64,3072]{2,1,0:T(8,128)(2,1)S(1)}, bf16[4,64,3072]{2,1,0:T(8,128)(2,1)}, u32[]{:S(2)}) copy-start(bf16[4,64,3072]{2,1,0:T(8,128)(2,1)} %param.16) | copy-start | bytes 4718596
  13.2 9.8 all-to-all-start.1
  23.0 11.5 all-to-all-start
  26.5 2191.4 %all-reduce.7.cloned.1.call-start = ((), (), s32[]{:S(2)}) async-start(), calls=%async_computation.10 | async-start | bytes 75497472
  345.8 1.7 copy-start.5
  406.8 3048.2 %all-reduce.5.cloned.1.call-start = ((), (), s32[]{:S(2)}) async-start(), calls=%async_computation.9 | async-start | bytes 75497472
  466.9 3606.3 %reduce-scatter.2.cloned.1.call-start = ((), (), s32[]{:S(2)}) async-start(), calls=%async_computation.8 | async-start | bytes 47185920 | tf_op jit(solution)/shard_map/reduce_scatter | solution.py:52
  482.5 1.0 copy-start.6
  484.4 508.1 %all-to-all-start.3 = ((f32[4,8,8]{2,0,1:T(4,128)}), f32[4,8,8]{2,0,1:T(4,128)S(1)}, u32[]{:S(2)}, u32[]{:S(2)}) async-start(f32[4,8,8]{2,0,1:T(4,128)} %copy.34), calls=%async_computation.3 | async-start | bytes 32768 | tf_op jit(solution)/shard_map/all_to_all | solution.py:47
  670.6 325.5 %copy-start.9 = (u32[32]{0:T(128)S(1)}, u32[32]{0:T(128)}, u32[]{:S(2)}) copy-start(u32[32]{0:T(128)} %constant.113) | copy-start | bytes 388
  992.5 11.8 all-to-all-start.2
  3464.4 608.7 %copy-start.1 = (bf16[4,64,768]{2,1,0:T(8,128)(2,1)S(1)}, bf16[4,64,768]{2,1,0:T(8,128)(2,1)}, u32[]{:S(2)}) copy-start(bf16[4,64,768]{2,1,0:T(8,128)(2,1)} %param.15) | copy-start | bytes 1179652
Sparse Core Ops, SparseCore 0:
  9.6 325.4 all-gather.3
  336.6 321.2 all-gather.5
  659.5 321.2 all-gather.7
  983.2 1234.5 all-reduce.6
  2220.2 1234.8 all-reduce.4
  3457.8 615.2 reduce-scatter.1
where the time goes:
time: 4080 us
  waiting for transfers between devices  3820 us (94%)
  local copies, waits for them, and re-layouts  146 us (4%)
  matrix products  80 us (2%)
    unnamed x8, waiting for transfers between devices  2430 us
    reduce_scatter x1, waiting for transfers between devices, local_backward(): lax.psum_scatter(dw_down, 'fsdp', scatter_dimension=1, tiled=True)  596 us
    all_gather x1, waiting for transfers between devices, local_backward(): full_w_up = lax.all_gather(w_up, 'fsdp', axis=1, tiled=True)  310 us
    all_gather x1, waiting for transfers between devices, local_backward(): full_w_down = lax.all_gather(w_down, 'fsdp', axis=1, tiled=True)  301 us
    all_gather x1, waiting for transfers between devices, local_backward(): full_w_gate = lax.all_gather(w_gate, 'fsdp', axis=1, tiled=True)  170 us
  transfers between devices with their start and end apart: 10, of which 9 were waited for; matrix products, arithmetic and copies ran while one was open for 6% of the time, Pallas kernels for 0%

commit v1 on v0

v1 whole, which is shorter than its diff:
```python
import jax
import jax.numpy as jnp
from jax import lax
from jax.sharding import PartitionSpec as P


def solution(mesh):
    ep_n = mesh.shape['ep']
    fs_n = mesh.shape['fsdp']
    tok_spec = P(('fsdp', 'ep'), None)
    row_spec = P('ep', 'fsdp', None)

    def local_backward(grad_out, expert_idx, slot_pos, gates, x_disp, h_gate, h_up, y_disp, w_gate, w_down, w_up):
        tok_n, top_n = expert_idx.shape
        e_loc, rows_loc, width = x_disp.shape
        hidden = h_gate.shape[2]
        f_loc = hidden // fs_n
        d_loc = width // fs_n
        slot_cap = rows_loc // ep_n
        slots_n = e_loc * ep_n * slot_cap
        choices = tok_n * top_n
        f32, bf16 = jnp.float32, jnp.bfloat16
        h_both = jnp.stack([h_gate, h_up]).reshape(2, e_loc, rows_loc, fs_n, f_loc).transpose(3, 0, 1, 2, 4)
        h_all = lax.all_to_all(h_both, 'fsdp', 0, 0, tiled=True)
        x_split = x_disp.reshape(e_loc, rows_loc, fs_n, d_loc).transpose(2, 0, 1, 3)
        x_all = lax.all_to_all(x_split, 'fsdp', 0, 0, tiled=True)
        send_row = jnp.where(slot_pos >= 0, ((expert_idx // e_loc) * e_loc + expert_idx % e_loc) * slot_cap + slot_pos, slots_n).reshape(-1)
        src_choice = jnp.full((slots_n,), choices, jnp.int32).at[send_row].set(jnp.arange(choices, dtype=jnp.int32), mode='drop')
        send_dy = jnp.take(grad_out, src_choice // top_n, axis=0, mode='fill', fill_value=0).reshape(ep_n, e_loc * slot_cap, width)
        send_gate = jnp.take(gates.reshape(-1), src_choice, mode='fill', fill_value=0).reshape(ep_n, e_loc * slot_cap)
        recv_dy = lax.all_to_all(send_dy, 'ep', 0, 0, tiled=True).reshape(ep_n, e_loc, slot_cap, width).transpose(1, 0, 2, 3).reshape(e_loc, rows_loc, width)
        recv_gate = lax.all_to_all(send_gate, 'ep', 0, 0, tiled=True).reshape(ep_n, e_loc, slot_cap).transpose(1, 0, 2).reshape(e_loc, rows_loc)
        g_rows = (recv_dy.astype(f32) * recv_gate[..., None]).astype(bf16)
        dgate_rows = jnp.sum(recv_dy.astype(f32) * y_disp.astype(f32), axis=2)
        back_gate = lax.all_to_all(dgate_rows.reshape(e_loc, ep_n, slot_cap).transpose(1, 0, 2), 'ep', 0, 0, tiled=True).reshape(slots_n)
        g_all = lax.all_gather(g_rows, 'fsdp', axis=0)
        g_all = g_all.transpose(1, 0, 2, 3).reshape(e_loc, fs_n * rows_loc, width)
        d_act = jnp.einsum('erd,efd->erf', g_all, w_down, preferred_element_type=f32)
        h_rows = h_all.transpose(1, 2, 0, 3, 4).reshape(2, e_loc, fs_n * rows_loc, f_loc)
        gate_pre = h_rows[0].astype(f32)
        up_pre = h_rows[1].astype(f32)
        sig = jax.nn.sigmoid(gate_pre)
        silu = gate_pre * sig
        act = (silu * up_pre).astype(bf16)
        dh_gate = (d_act * up_pre * sig * (1.0 + gate_pre * (1.0 - sig))).astype(bf16)
        dh_up = (d_act * silu).astype(bf16)
        grad_w_down = jnp.einsum('erf,erd->efd', act, g_all, preferred_element_type=f32)
        dh_all = lax.all_gather(jnp.stack([dh_gate, dh_up]), 'fsdp', axis=0)
        x_rows = x_all.transpose(1, 0, 2, 3).reshape(e_loc, fs_n * rows_loc, d_loc)
        dh_g = dh_all[:, 0]
        dh_u = dh_all[:, 1]
        grad_w_gate = jnp.einsum('erd,serf->edsf', x_rows, dh_g, preferred_element_type=f32).reshape(e_loc, d_loc, hidden)
        grad_w_up = jnp.einsum('erd,serf->edsf', x_rows, dh_u, preferred_element_type=f32).reshape(e_loc, d_loc, hidden)
        wg = w_gate.reshape(e_loc, d_loc, fs_n, f_loc)
        wu = w_up.reshape(e_loc, d_loc, fs_n, f_loc)
        dx = (jnp.einsum('serf,edsf->erd', dh_g, wg, preferred_element_type=f32) + jnp.einsum('serf,edsf->erd', dh_u, wu, preferred_element_type=f32)).astype(bf16)
        dx_send = dx.reshape(e_loc, fs_n * ep_n, slot_cap, d_loc).transpose(1, 0, 2, 3)
        dx_back = lax.all_to_all(dx_send, ('fsdp', 'ep'), 0, 0, tiled=True)
        dx_back = dx_back.reshape(fs_n, slots_n, d_loc).transpose(1, 0, 2).reshape(slots_n, width)
        picked = jnp.take(dx_back, send_row, axis=0, mode='fill', fill_value=0).reshape(tok_n, top_n, width)
        grad_x = jnp.sum(picked.astype(f32), axis=1).astype(bf16)
        grad_gates = jnp.take(back_gate, send_row, mode='fill', fill_value=0).reshape(tok_n, top_n)
        return grad_x, grad_gates, grad_w_gate, grad_w_down, grad_w_up

    return jax.shard_map(local_backward, mesh=mesh, in_specs=(tok_spec, tok_spec, tok_spec, tok_spec, row_spec, row_spec, row_spec, row_spec, row_spec, row_spec, row_spec), out_specs=(tok_spec, tok_spec, row_spec, row_spec, row_spec), check_vma=False)
```

time: 4080 us -> 424 us (0.10)
  waiting for transfers between devices: 3820 us -> 303 us
  local copies, waits for them, and re-layouts: 146 us -> 37.4 us
  matrix products: 80 us -> 32.7 us
    unnamed x8 -> x2, waiting for transfers between devices: 2430 us -> 0.03 us
    all_gather x3 -> x2, waiting for transfers between devices: 781 us -> 180 us  [the longest x1 180 us: local_backward(): dh_all = lax.all_gather(jnp.stack([dh_gate, dh_up]), 'fsdp', axis=0)]
    reduce_scatter x1 -> x0, waiting for transfers between devices: 596 us -> none  [local_backward(): lax.psum_scatter(dw_down, 'fsdp', scatter_dimension=1, tiled=True)]
    all_to_all x4 -> x6, waiting for transfers between devices: 15.1 us -> 123 us  [the longest x1 92.9 us: local_backward(): h_all = lax.all_to_all(h_both, 'fsdp', 0, 0, tiled=True)]
    dot_general x2 -> x0, local copies, waits for them, and re-layouts: 89.2 us -> none  [the longest x1 44.6 us: expert_grads(): jnp.einsum('erd,erf->edf', x_rows, dh_gate, preferred_element_type=jnp.fl...]
    dot_general x6, matrix products: 80 us -> 32.7 us  [the longest x1 8.59 us: local_backward(): jnp.einsum('erf,erd->efd', act, g_all, preferred_element_type=f32)]
    unnamed x25 -> x20, local copies, waits for them, and re-layouts: 48.2 us -> 1.02 us
  transfers between devices with their start and end apart: 10 -> 8, of which waited for: 9 -> 5; matrix products, arithmetic and copies ran while one was open for 6% -> 11% of each run, Pallas kernels for 0% -> 0%
where the time goes in v1:
time: 424 us; the launch traced here: 423 us
  waiting for transfers between devices  303 us (71%)
  local copies, waits for them, and re-layouts  37.4 us (9%)
  matrix products  32.7 us (8%)
  starting transfers between devices  24.7 us (6%)
  between operations  14.3 us (3%)
  other arithmetic  11.6 us (3%)
    all_gather x1, waiting for transfers between devices, local_backward(): dh_all = lax.all_gather(jnp.stack([dh_gate, dh_up]), 'fsdp', axis=0)  180 us
    all_to_all x1, waiting for transfers between devices, local_backward(): h_all = lax.all_to_all(h_both, 'fsdp', 0, 0, tiled=True)  92.9 us
    all_to_all x1, waiting for transfers between devices, local_backward(): x_all = lax.all_to_all(x_split, 'fsdp', 0, 0, tiled=True)  24.6 us
    dot_general x1, matrix products, local_backward(): jnp.einsum('erf,erd->efd', act, g_all, preferred_element_type=f32)  8.59 us
  transfers between devices with their start and end apart: 8, of which 5 were waited for; matrix products, arithmetic and copies ran while one was open for 11% of the time, Pallas kernels for 0%

profile of v1, /device:TPU:0, one launch (start us, length us, event | category | flops | bytes accessed | tf_op | source)
XLA Modules:
  0.0 423.3 jit_solution(14889490814514218912)
XLA Ops:
  7.2 0.0 copy-start
  7.2 0.8 fusion.33
  8.0 1.0 scatter_custom_fusion
  9.0 1.9 gather_fusion.1
  10.9 0.7 select_n.73
  11.6 5.2 %all-to-all-start.1 = ((f32[8,1,32]{2,1,0:T(1,128)}), f32[8,1,32]{2,1,0:T(1,128)S(1)}, u32[]{:S(2)}, u32[]{:S(2)}) async-start(f32[8,1,32]{2,1,0:T(1,128)} %select_n.73), calls=%async_computation.1 | async-start | bytes 8192 | tf_op jit(solution)/shard_map/all_to_all | solution.py:32
  16.9 0.1 broadcast_in_dim.50
  16.9 1.2 gather_fusion
  18.1 0.9 broadcast_select_fusion
  19.0 2.4 all-to-all-done.1
  21.4 4.1 all-to-all-start
  25.5 1.2 stack.18
  26.7 3.3 stack.19
  30.0 2.2 maximum_bitcast_fusion
  32.2 2.2 copy.80
  34.5 0.0 all-to-all-done
  34.5 4.9 %all-to-all-start.2 = ((bf16[4,2,4,64,768]{4,3,2,1,0:T(8,128)(2,1)}), bf16[4,2,4,64,768]{4,3,2,1,0:T(8,128)(2,1)S(1)}, u32[]{:S(2)}, u32[]{:S(2)}) async-start(bf16[4,2,4,64,768]{4,3,2,1,0:T(8,128)(2,1)} %copy.80), calls=%async_computation.2 | async-start | bytes 6291456 | tf_op jit(solution)/shard_map/all_to_all | solution.py:24
  39.3 0.5 broadcast.84
  39.9 0.7 reduce.3
  40.5 0.1 reshape.153
  40.6 0.1 mul.54
  40.7 1.9 fusion.27
  42.6 0.0 all-gather.4.cloned.1.call-update
  42.6 0.0 all-gather.6.cloned.1.call-start
  42.6 92.9 %all-to-all-done.2 = bf16[4,2,4,64,768]{4,3,2,1,0:T(8,128)(2,1)S(1)} async-done(((bf16[4,2,4,64,768]{4,3,2,1,0:T(8,128)(2,1)}), bf16[4,2,4,64,768]{4,3,2,1,0:T(8,128)(2,1)S(1)}, u32[]{:S(2)}, u32[]{:S(2)}) %all-to-all-start.2) | async-done | bytes 3145760 | tf_op jit(solution)/shard_map/all_to_all | solution.py:24
  135.5 0.8 slice_convert_fusion.1
  136.3 0.3 copy.81
  136.6 2.2 copy.82
  138.8 5.7 %fusion.13 = (bf16[1,4,256,768]{3,2,1,0:T(8,128)(2,1)S(1)}, bf16[1,4,256,768]{3,2,1,0:T(8,128)(2,1)S(1)}) fusion(f32[4,256,768]{2,1,0:T(8,128)} %bitcast.123, f32[4,256,768]{2,1,0:T(8,128)S(1)} %bitcast.121, bf16[4,256,768]{2,1,0:T(8,128)(2,1)} %bitcast.137, bf16[4,768,768]{2,1,0:T(8,128)(2,1)} %param.20), kind=kOutput, calls=%fused_computation.28 | convolution fusion | flops 1218183168 | bytes 15728640 | tf_op jit(solution)/shard_map/erd,efd->erf/dot_general | solution.py:38
  144.5 1.9 pad_maximum_fusion
  146.5 0.0 all-gather.6.cloned.1.call-update
  146.5 1.0 copy-done.7
  147.4 1.2 fusion.26
  148.6 0.1 reshape.160
  148.7 0.6 copy.91
  149.3 3.8 all-to-all-start.4
  153.1 0.5 reshape.162
  153.6 0.9 copy.92
  154.5 3.2 all-to-all-done.4
  157.7 3.7 all-to-all-start.5
  161.3 0.1 reshape.161
  161.4 1.3 gather_fusion.3
  162.7 0.5 bitcast_select_fusion
  163.2 24.6 %all-to-all-done.5 = bf16[4,4,64,192]{3,2,1,0:T(8,128)(2,1)S(1)} async-done(((bf16[4,4,64,192]{3,2,1,0:T(8,128)(2,1)}), bf16[4,4,64,192]{3,2,1,0:T(8,128)(2,1)S(1)}, u32[]{:S(2)}, u32[]{:S(2)}) %all-to-all-start.5) | async-done | bytes 393248 | tf_op jit(solution)/shard_map/all_to_all | solution.py:26
  187.9 8.6 %fusion.12 = f32[4,768,768]{2,1,0:T(8,128)} fusion(bf16[4,256,768]{2,1,0:T(8,128)(2,1)} %bitcast.138, f32[4,256,768]{2,1,0:T(8,128)} %bitcast.122, f32[4,256,768]{2,1,0:T(8,128)} %bitcast.124), kind=kOutput, calls=%fused_computation.25 | convolution fusion | flops 1212678144 | bytes 17301504 | tf_op jit(solution)/shard_map/erf,erd->efd/dot_general | solution.py:47
  196.5 179.5 %all-gather.6.cloned.1.call-done = bf16[8,4,256,768]{3,2,1,0:T(8,128)(2,1)} async-done(((bf16[2,4,256,768]{3,2,1,0:T(8,128)(2,1)}), bf16[8,4,256,768]{3,2,1,0:T(8,128)(2,1)}) %all-gather.6.cloned.1.call-update) | async-done | bytes 12582928 | tf_op jit(solution)/shard_map/all_gather | solution.py:48
  376.0 5.5 %fusion.34 = (bf16[4,1,4,256,768]{4,3,2,1,0:T(8,128)(2,1)S(1)}, bf16[4,1,4,256,768]{4,3,2,1,0:T(8,128)(2,1)S(1)}) fusion(bf16[4,2,4,256,768]{4,3,2,1,0:T(8,128)(2,1)} %bitcast.115), kind=kLoop, calls=%fused_computation.59 | loop fusion | bytes 25165824 | tf_op jit(solution)/shard_map/slice | solution.py:50
  381.6 0.0 copy-start.3
  381.6 8.0 %fusion.14 = f32[4,256,192]{1,2,0:T(8,128)S(1)} fusion(bf16[4,24,4,8,768]{4,3,2,1,0:T(8,128)(2,1)} %bitcast.135, bf16[4,1,4,256,768]{4,3,2,1,0:T(8,128)(2,1)S(1)} %get-tuple-element.10), kind=kOutput, calls=%fused_computation.29 | convolution fusion | flops 1207959552 | bytes 11796480 | tf_op jit(solution)/shard_map/serf,edsf->erd/dot_general | solution.py:56
  389.6 4.6 %fusion.23 = bf16[4,256,192]{1,2,0:T(8,128)(2,1)S(1)} fusion(f32[4,256,192]{1,2,0:T(8,128)S(1)} %fusion.14, bf16[4,24,4,8,768]{4,3,2,1,0:T(8,128)(2,1)} %bitcast.136, bf16[4,1,4,256,768]{4,3,2,1,0:T(8,128)(2,1)S(1)} %get-tuple-element.9), kind=kOutput, calls=%fused_computation.32 | convolution fusion | flops 1208352768 | bytes 12189696 | tf_op jit(solution)/shard_map/serf,edsf->erd/dot_general | solution.py:56
  394.2 0.2 copy.87
  394.4 0.9 copy.88
  395.3 3.0 all-to-all-start.3
  398.3 0.0 slice-start.1
  398.3 4.4 %fusion.9 = f32[4,4,24,8,768]{4,3,2,1,0:T(8,128)S(1)} fusion(bf16[4,256,192,1]{2,1,3,0:T(8,128)(2,1)S(1)} %bitcast.119, bf16[4,1,4,256,768]{4,3,2,1,0:T(8,128)(2,1)} %copy-done.3), kind=kOutput, calls=%fused_computation.16 | convolution fusion | flops 1207959552 | bytes 16121856 | tf_op jit(solution)/shard_map/erd,serf->edsf/dot_general | solution.py:52
  402.6 5.2 %copy.112 = f32[4,4,24,8,768]{4,3,1,2,0:T(8,128)} copy(f32[4,4,24,8,768]{4,3,2,1,0:T(8,128)S(1)} %fusion.9) | data formatting | bytes 18874368 | tf_op jit(solution)/shard_map/reshape | solution.py:52
  407.8 1.4 fusion.8
  409.3 0.0 copy-start.1
  409.3 5.2 %copy.113 = f32[4,4,24,8,768]{4,3,1,2,0:T(8,128)} copy(f32[4,4,24,8,768]{4,3,2,1,0:T(8,128)S(1)} %fusion.8) | data formatting | bytes 18874368 | tf_op jit(solution)/shard_map/reshape | solution.py:53
  414.5 0.0 all-to-all-done.3
  414.5 0.2 copy.89
  414.7 0.2 copy.90
  414.8 0.9 gather_fusion.2
  415.7 0.8 broadcast_select_fusion.1
  (25 shorter events, 0.1 us)
Async XLA Ops:
  7.2 9.8 %copy-start = (bf16[128,768]{1,0:T(8,128)(2,1)S(1)}, bf16[128,768]{1,0:T(8,128)(2,1)}, u32[]{:S(2)}) copy-start(bf16[128,768]{1,0:T(8,128)(2,1)} %param.11) | copy-start | bytes 589828
  7.2 18.3 %copy-start.5 = (bf16[4,64,3072]{2,1,0:T(8,128)(2,1)S(1)}, bf16[4,64,3072]{2,1,0:T(8,128)(2,1)}, u32[]{:S(2)}) copy-start(bf16[4,64,3072]{2,1,0:T(8,128)(2,1)} %param.16) | copy-start | bytes 4718596
  11.6 9.7 %all-to-all-start.1 = ((f32[8,1,32]{2,1,0:T(1,128)}), f32[8,1,32]{2,1,0:T(1,128)S(1)}, u32[]{:S(2)}, u32[]{:S(2)}) async-start(f32[8,1,32]{2,1,0:T(1,128)} %select_n.73), calls=%async_computation.1 | async-start | bytes 8192 | tf_op jit(solution)/shard_map/all_to_all | solution.py:32
  21.4 13.1 %all-to-all-start = ((bf16[8,32,768]{2,1,0:T(8,128)(2,1)}), bf16[8,32,768]{2,1,0:T(8,128)(2,1)}, u32[]{:S(2)}, u32[]{:S(2)}) async-start(bf16[8,32,768]{2,1,0:T(8,128)(2,1)} %broadcast_select_fusion), calls=%async_computation | async-start | bytes 786432 | tf_op jit(solution)/shard_map/all_to_all | solution.py:31
  34.5 101.1 %all-to-all-start.2 = ((bf16[4,2,4,64,768]{4,3,2,1,0:T(8,128)(2,1)}), bf16[4,2,4,64,768]{4,3,2,1,0:T(8,128)(2,1)S(1)}, u32[]{:S(2)}, u32[]{:S(2)}) async-start(bf16[4,2,4,64,768]{4,3,2,1,0:T(8,128)(2,1)} %copy.80), calls=%async_computation.2 | async-start | bytes 6291456 | tf_op jit(solution)/shard_map/all_to_all | solution.py:24
  39.3 99.5 %all-gather.4.cloned.1.call-start = ((), (), s32[]{:S(2)}) async-start(), calls=%async_computation.6 | async-start | bytes 1966080 | tf_op jit(solution)/shard_map/all_gather | solution.py:36
  42.6 333.4 %all-gather.6.cloned.1.call-start = ((), (), s32[]{:S(2)}) async-start(), calls=%async_computation.7 | async-start | bytes 15728640 | tf_op jit(solution)/shard_map/all_gather | solution.py:48
  136.6 7.9 %copy-start.4 = (f32[1,4,4,64,768]{4,3,2,1,0:T(8,128)}, f32[1,4,4,64,768]{4,3,2,1,0:T(8,128)S(1)}, u32[]{:S(2)}) copy-start(f32[1,4,4,64,768]{4,3,2,1,0:T(8,128)S(1)} %copy.81) | copy-start | bytes 9437188
  146.5 1.0 copy-start.7
  146.5 6.7 %copy-start.6 = (bf16[4,64,768]{2,1,0:T(8,128)(2,1)S(1)}, bf16[4,64,768]{2,1,0:T(8,128)(2,1)}, u32[]{:S(2)}) copy-start(bf16[4,64,768]{2,1,0:T(8,128)(2,1)} %param.15) | copy-start | bytes 1179652
  149.3 8.3 %all-to-all-start.4 = ((f32[8,4,8]{2,1,0:T(4,128)}), f32[8,4,8]{2,1,0:T(4,128)S(1)}, u32[]{:S(2)}, u32[]{:S(2)}) async-start(f32[8,4,8]{2,1,0:T(4,128)} %copy.91), calls=%async_computation.4 | async-start | bytes 32768 | tf_op jit(solution)/shard_map/all_to_all | solution.py:35
  157.7 30.2 %all-to-all-start.5 = ((bf16[4,4,64,192]{3,2,1,0:T(8,128)(2,1)}), bf16[4,4,64,192]{3,2,1,0:T(8,128)(2,1)S(1)}, u32[]{:S(2)}, u32[]{:S(2)}) async-start(bf16[4,4,64,192]{3,2,1,0:T(8,128)(2,1)} %copy.92), calls=%async_computation.5 | async-start | bytes 1048576 | tf_op jit(solution)/shard_map/all_to_all | solution.py:26
  381.6 8.1 %copy-start.2 = (bf16[4,1,4,256,768]{4,3,2,1,0:T(8,128)(2,1)}, bf16[4,1,4,256,768]{4,3,2,1,0:T(8,128)(2,1)S(1)}, u32[]{:S(2)}) copy-start(bf16[4,1,4,256,768]{4,3,2,1,0:T(8,128)(2,1)S(1)} %get-tuple-element.10) | copy-start | bytes 18874372
  381.6 8.1 %copy-start.3 = (bf16[4,1,4,256,768]{4,3,2,1,0:T(8,128)(2,1)}, bf16[4,1,4,256,768]{4,3,2,1,0:T(8,128)(2,1)S(1)}, u32[]{:S(2)}) copy-start(bf16[4,1,4,256,768]{4,3,2,1,0:T(8,128)(2,1)S(1)} %get-tuple-element.9) | copy-start | bytes 18874372
  395.3 12.5 %slice-start = ((s8[6291456]{0:T(1024)(128)(4,1)}), s8[2097152]{0:T(1024)(128)(4,1)S(1)}, s32[]{:S(2)}) async-start(s8[6291456]{0:T(1024)(128)(4,1)} %bitcast.113), calls=%async_computation.8 | async-start | bytes 4194304
  395.3 19.2 %all-to-all-start.3 = ((bf16[32,4,8,192]{3,2,1,0:T(8,128)(2,1)}), bf16[32,4,8,192]{3,2,1,0:T(8,128)(2,1)S(1)}, u32[]{:S(2)}, u32[]{:S(2)}) async-start(bf16[32,4,8,192]{3,2,1,0:T(8,128)(2,1)} %copy.88), calls=%async_computation.3 | async-start | bytes 1048576 | tf_op jit(solution)/shard_map/all_to_all | solution.py:58
  398.3 9.6 %slice-start.1 = ((s8[6291456]{0:T(1024)(128)(4,1)}), s8[4194304]{0:T(1024)(128)(4,1)S(1)}, s32[]{:S(2)}) async-start(s8[6291456]{0:T(1024)(128)(4,1)} %bitcast.113), calls=%async_computation.9 | async-start | bytes 8388608
  409.3 7.2 %copy-start.1 = (bf16[128,768]{1,0:T(8,128)(2,1)S(1)}, bf16[128,768]{1,0:T(8,128)(2,1)}, u32[]{:S(2)}) copy-start(bf16[128,768]{1,0:T(8,128)(2,1)} %param.11) | copy-start | bytes 589828
Sparse Core Ops, SparseCore 0:
  42.7 60.6 all-gather.3
  146.6 229.3 all-gather.5

commit v2 on v1

v2 whole, which is shorter than its diff:
```python
import functools

import jax
import jax.numpy as jnp
from jax import lax
from jax.experimental import pallas as pl
from jax.experimental.pallas import tpu as pltpu
from jax.sharding import PartitionSpec as P

MESH = pl.DeviceIdType.MESH
F32, BF16 = jnp.float32, jnp.bfloat16
ANY = pl.BlockSpec(memory_space=pl.ANY)
VMEM = pl.BlockSpec(memory_space=pltpu.VMEM)


def remote(src, dst, send, recv, device):
    return pltpu.make_async_remote_copy(src_ref=src, dst_ref=dst, send_sem=send, recv_sem=recv, device_id=device, device_id_type=MESH)


def exchange_kernel(fs_n, ep_n, hg, hu, xs, dy_s, gt_s, y, h_all, x_all, g_all, dg_back, dy_r, gt_r, g_own, dg_own, h_ss, h_rs, x_ss, x_rs, d_ss, d_rs, t_ss, t_rs, g_ss, g_rs, b_ss, b_rs, l_sem):
    q = lax.axis_index('fsdp')
    p = lax.axis_index('ep')
    f_loc = h_all.shape[-1]
    barrier = pltpu.get_barrier_semaphore()
    zs = [lax.rem(q + k, fs_n) for k in range(1, fs_n)]
    es = [lax.rem(p + k, ep_n) for k in range(1, ep_n)]
    for z in zs:
        pl.semaphore_signal(barrier, inc=1, device_id={'fsdp': z}, device_id_type=MESH)
    for e in es:
        pl.semaphore_signal(barrier, inc=1, device_id={'ep': e}, device_id_type=MESH)
    pl.semaphore_wait(barrier, fs_n + ep_n - 2)
    d_copies = []
    for k, e in enumerate(es):
        d_copies.append(remote(dy_s.at[e], dy_r.at[:, p], d_ss.at[k], d_rs.at[k], {'ep': e}))
        d_copies.append(remote(gt_s.at[e], gt_r.at[:, p], t_ss.at[k], t_rs.at[k], {'ep': e}))
    for c in d_copies:
        c.start()
    l_d = pltpu.make_async_copy(dy_s.at[p], dy_r.at[:, p], l_sem.at[0])
    l_t = pltpu.make_async_copy(gt_s.at[p], gt_r.at[:, p], l_sem.at[1])
    l_d.start()
    l_t.start()
    h_copies = []
    for k, z in enumerate(zs):
        cols = pl.ds(pl.multiple_of(z * f_loc, 128), f_loc)
        h_copies.append(remote(hg.at[:, :, cols], h_all.at[0, :, q], h_ss.at[0, k], h_rs.at[0, k], {'fsdp': z}))
        h_copies.append(remote(hu.at[:, :, cols], h_all.at[1, :, q], h_ss.at[1, k], h_rs.at[1, k], {'fsdp': z}))
        h_copies.append(remote(xs.at[z], x_all.at[:, q], x_ss.at[k], x_rs.at[k], {'fsdp': z}))
    for c in h_copies:
        c.start()
    cols = pl.ds(pl.multiple_of(q * f_loc, 128), f_loc)
    locals_ = [
        pltpu.make_async_copy(hg.at[:, :, cols], h_all.at[0, :, q], l_sem.at[2]),
        pltpu.make_async_copy(hu.at[:, :, cols], h_all.at[1, :, q], l_sem.at[3]),
        pltpu.make_async_copy(xs.at[q], x_all.at[:, q], l_sem.at[4]),
    ]
    for c in locals_:
        c.start()
    l_d.wait()
    l_t.wait()
    for c in d_copies:
        c.wait()
    e_loc, _, cap, width = dy_r.shape

    def body(i, carry):
        e = i // ep_n
        s = i % ep_n
        gate = gt_r[e, s]
        acc = jnp.zeros((cap, 128), F32)
        for k in range(width // 128):
            sl = slice(k * 128, (k + 1) * 128)
            dy = dy_r[e, s, :, sl].astype(F32)
            g_own[e, s, :, sl] = (dy * gate).astype(BF16)
            acc = acc + dy * y[e, s, :, sl].astype(F32)
        dg_own[s, e] = jnp.broadcast_to(jnp.sum(acc, axis=1, keepdims=True), (cap, 128))
        return carry

    lax.fori_loop(0, e_loc * ep_n, body, 0)
    g_copies = []
    for k, z in enumerate(zs):
        g_copies.append(remote(g_own, g_all.at[:, q], g_ss.at[k], g_rs.at[k], {'fsdp': z}))
    for k, e in enumerate(es):
        g_copies.append(remote(dg_own.at[e], dg_back.at[p], b_ss.at[k], b_rs.at[k], {'ep': e}))
    for c in g_copies:
        c.start()
    l_g = pltpu.make_async_copy(g_own, g_all.at[:, q], l_sem.at[5])
    l_b = pltpu.make_async_copy(dg_own.at[p], dg_back.at[p], l_sem.at[6])
    l_g.start()
    l_b.start()
    for c in locals_:
        c.wait()
    l_g.wait()
    l_b.wait()
    for c in h_copies:
        c.wait()
    for c in g_copies:
        c.wait()


def gather_kernel(fs_n, dh, dh_all, s1, r1, s2, r2, l_sem):
    q = lax.axis_index('fsdp')
    right = lax.rem(q + 1, fs_n)
    left = lax.rem(q + fs_n - 1, fs_n)
    e_loc = dh.shape[1]
    barrier = pltpu.get_barrier_semaphore()
    for z in (left, right):
        pl.semaphore_signal(barrier, inc=1, device_id={'fsdp': z}, device_id_type=MESH)
    pl.semaphore_wait(barrier, 2)
    to_right, to_left = {}, {}
    for t in range(2):
        for e in range(e_loc):
            u = 1 - t
            to_right[t, e] = remote(dh.at[t, e], dh_all.at[q, t, e], s1.at[0, t, e], r1.at[0, t, e], {'fsdp': right})
            to_right[t, e].start()
            to_left[u, e] = remote(dh.at[u, e], dh_all.at[q, u, e], s1.at[1, u, e], r1.at[1, u, e], {'fsdp': left})
            to_left[u, e].start()
    own = pltpu.make_async_copy(dh, dh_all.at[q], l_sem)
    own.start()
    fwd = []
    for e in range(e_loc):
        to_right[0, e].wait_recv()
        c = remote(dh_all.at[left, 0, e], dh_all.at[left, 0, e], s2.at[0, e], r2.at[0, e], {'fsdp': right})
        c.start()
        fwd.append(c)
        to_left[1, e].wait_recv()
        c = remote(dh_all.at[right, 1, e], dh_all.at[right, 1, e], s2.at[1, e], r2.at[1, e], {'fsdp': left})
        c.start()
        fwd.append(c)
    own.wait()
    for e in range(e_loc):
        to_right[1, e].wait_recv()
        to_left[0, e].wait_recv()
    for e in range(e_loc):
        for t in range(2):
            to_right[t, e].wait_send()
            to_left[t, e].wait_send()
    for c in fwd:
        c.wait()


def hidden_kernel(g, h, w, dh, act):
    d_act = lax.dot_general(g[0], w[0], (((1,), (1,)), ((), ())), preferred_element_type=F32)
    gate_pre = h[0, 0].astype(F32)
    up_pre = h[1, 0].astype(F32)
    sig = jax.nn.sigmoid(gate_pre)
    silu = gate_pre * sig
    act[0] = (silu * up_pre).astype(BF16)
    dh[0, 0] = (d_act * up_pre * sig * (1.0 + gate_pre * (1.0 - sig))).astype(BF16)
    dh[1, 0] = (d_act * silu).astype(BF16)


def dx_kernel(dh, wg, wu, dx, acc):
    s = pl.program_id(1)
    nt = (((1,), (1,)), ((), ()))
    term = lax.dot_general(dh[0, 0, 0], wg[0], nt, preferred_element_type=F32) + lax.dot_general(dh[0, 1, 0], wu[0], nt, preferred_element_type=F32)

    @pl.when(s == 0)
    def _():
        acc[...] = term

    @pl.when(s > 0)
    def _():
        acc[...] += term

    @pl.when(s == pl.num_programs(1) - 1)
    def _():
        dx[0] = acc[...].astype(BF16)


def dw_kernel(x, dh, act, g, dwg, dwu, dwd):
    tn = (((0,), (0,)), ((), ()))
    dwg[0] = lax.dot_general(x[0], dh[0, 0, 0], tn, preferred_element_type=F32)
    dwu[0] = lax.dot_general(x[0], dh[0, 1, 0], tn, preferred_element_type=F32)
    dwd[0] = lax.dot_general(act[0], g[0], tn, preferred_element_type=F32)


def solution(mesh):
    ep_n = mesh.shape['ep']
    fs_n = mesh.shape['fsdp']
    tok_spec = P(('fsdp', 'ep'), None)
    row_spec = P('ep', 'fsdp', None)

    def local_backward(grad_out, expert_idx, slot_pos, gates, x_disp, h_gate, h_up, y_disp, w_gate, w_down, w_up):
        tok_n, top_n = expert_idx.shape
        e_loc, rows_loc, width = x_disp.shape
        hidden = h_gate.shape[2]
        f_loc = hidden // fs_n
        d_loc = width // fs_n
        cap = rows_loc // ep_n
        slots_n = e_loc * ep_n * cap
        rows = fs_n * rows_loc
        dma = pltpu.SemaphoreType.DMA
        x_split = x_disp.reshape(e_loc, rows_loc, fs_n, d_loc).transpose(2, 0, 1, 3)
        dest = jnp.where(slot_pos >= 0, expert_idx * cap + slot_pos, slots_n)
        hit = dest[None, :, :] == lax.broadcasted_iota(jnp.int32, (slots_n, tok_n, top_n), 0)
        pick = jnp.sum(hit, axis=2).astype(BF16)
        send_dy = jnp.dot(pick, grad_out, preferred_element_type=F32).astype(BF16).reshape(ep_n, e_loc, cap, width)
        send_gate = jnp.sum(jnp.where(hit, gates[None], 0.0), axis=(1, 2))
        send_gate = jnp.broadcast_to(send_gate[:, None], (slots_n, 128)).reshape(ep_n, e_loc, cap, 128)
        h_all, x_all, g_all, dg_back = pl.pallas_call(
            functools.partial(exchange_kernel, fs_n, ep_n),
            out_shape=(
                jax.ShapeDtypeStruct((2, e_loc, fs_n, rows_loc, f_loc), BF16),
                jax.ShapeDtypeStruct((e_loc, fs_n, rows_loc, d_loc), BF16),
                jax.ShapeDtypeStruct((e_loc, fs_n, ep_n, cap, width), BF16),
                jax.ShapeDtypeStruct((ep_n, e_loc, cap, 128), F32),
            ),
            in_specs=[ANY, ANY, ANY, VMEM, VMEM, VMEM],
            out_specs=[ANY, ANY, ANY, VMEM],
            scratch_shapes=[
                pltpu.VMEM((e_loc, ep_n, cap, width), BF16),
                pltpu.VMEM((e_loc, ep_n, cap, 128), F32),
                pltpu.VMEM((e_loc, ep_n, cap, width), BF16),
                pltpu.VMEM((ep_n, e_loc, cap, 128), F32),
                dma((2, fs_n - 1)), dma((2, fs_n - 1)), dma((fs_n - 1,)), dma((fs_n - 1,)),
                dma((ep_n - 1,)), dma((ep_n - 1,)), dma((ep_n - 1,)), dma((ep_n - 1,)),
                dma((fs_n - 1,)), dma((fs_n - 1,)), dma((ep_n - 1,)), dma((ep_n - 1,)),
                dma((7,)),
            ],
            compiler_params=pltpu.CompilerParams(collective_id=0, has_side_effects=True),
            name='exchange',
        )(h_gate, h_up, x_split, send_dy, send_gate, y_disp.reshape(e_loc, ep_n, cap, width))
        g_rows = g_all.reshape(e_loc, rows, width)
        h_rows = h_all.reshape(2, e_loc, rows, f_loc)
        x_rows = x_all.reshape(e_loc, rows, d_loc)
        dh, act = pl.pallas_call(
            hidden_kernel,
            grid=(e_loc,),
            out_shape=(jax.ShapeDtypeStruct((2, e_loc, rows, f_loc), BF16), jax.ShapeDtypeStruct((e_loc, rows, f_loc), BF16)),
            in_specs=[
                pl.BlockSpec((1, rows, width), lambda e: (e, 0, 0)),
                pl.BlockSpec((2, 1, rows, f_loc), lambda e: (0, e, 0, 0)),
                pl.BlockSpec((1, f_loc, width), lambda e: (e, 0, 0)),
            ],
            out_specs=[
                pl.BlockSpec((2, 1, rows, f_loc), lambda e: (0, e, 0, 0)),
                pl.BlockSpec((1, rows, f_loc), lambda e: (e, 0, 0)),
            ],
            name='hidden',
        )(g_rows, h_rows, w_down)
        dh_all = pl.pallas_call(
            functools.partial(gather_kernel, fs_n),
            out_shape=jax.ShapeDtypeStruct((fs_n, 2, e_loc, rows, f_loc), BF16),
            in_specs=[ANY],
            out_specs=ANY,
            scratch_shapes=[dma((2, 2, e_loc)), dma((2, 2, e_loc)), dma((2, e_loc)), dma((2, e_loc)), dma],
            compiler_params=pltpu.CompilerParams(collective_id=1, has_side_effects=True),
            name='gather',
        )(dh)
        dh_spec = pl.BlockSpec((1, 2, 1, rows, f_loc), lambda e, s: (s, 0, e, 0, 0))
        w_spec = pl.BlockSpec((1, d_loc, f_loc), lambda e, s: (e, 0, s))
        dx = pl.pallas_call(
            dx_kernel,
            grid=(e_loc, fs_n),
            out_shape=jax.ShapeDtypeStruct((e_loc, rows, d_loc), BF16),
            in_specs=[dh_spec, w_spec, w_spec],
            out_specs=pl.BlockSpec((1, rows, d_loc), lambda e, s: (e, 0, 0)),
            scratch_shapes=[pltpu.VMEM((rows, d_loc), F32)],
            name='dx',
        )(dh_all, w_gate, w_up)
        dx_send = dx.reshape(e_loc, fs_n * ep_n, cap, d_loc).transpose(1, 0, 2, 3)
        dx_back = lax.all_to_all(dx_send, ('fsdp', 'ep'), 0, 0, tiled=True)
        piece = slots_n // fs_n
        rows_spec = pl.BlockSpec((1, rows, f_loc // fs_n), lambda e, s: (e, 0, s))
        grad_w_gate, grad_w_up, grad_w_down = pl.pallas_call(
            dw_kernel,
            grid=(e_loc, fs_n),
            out_shape=(
                jax.ShapeDtypeStruct((e_loc, d_loc, hidden), F32),
                jax.ShapeDtypeStruct((e_loc, d_loc, hidden), F32),
                jax.ShapeDtypeStruct((e_loc, f_loc, width), F32),
            ),
            in_specs=[
                pl.BlockSpec((1, rows, d_loc), lambda e, s: (e, 0, 0)),
                dh_spec,
                pl.BlockSpec((1, rows, f_loc), lambda e, s: (e, 0, 0)),
                pl.BlockSpec((1, rows, width // 3), lambda e, s: (e, 0, jnp.minimum(s, 2))),
            ],
            out_specs=[w_spec, w_spec, pl.BlockSpec((1, f_loc, width // 3), lambda e, s: (e, 0, jnp.minimum(s, 2)))],
            cost_estimate=pl.CostEstimate(flops=2 * e_loc * rows * hidden * width, bytes_accessed=50_000_000, transcendentals=0),
            name='dw',
        )(x_rows, dh_all, act, g_rows)
        back = dx_back.reshape(fs_n, slots_n, d_loc).transpose(1, 0, 2).reshape(slots_n, width)
        picked = lax.dot_general(pick, back, (((0,), (0,)), ((), ())), preferred_element_type=F32)
        grad_x = picked.astype(BF16)
        grad_gates = jnp.sum(jnp.where(hit, dg_back.reshape(slots_n, 128)[:, 0][:, None, None], 0.0), axis=0)
        return grad_x, grad_gates, grad_w_gate, grad_w_down, grad_w_up

    return jax.shard_map(local_backward, mesh=mesh, in_specs=(tok_spec, tok_spec, tok_spec, tok_spec, row_spec, row_spec, row_spec, row_spec, row_spec, row_spec, row_spec), out_specs=(tok_spec, tok_spec, row_spec, row_spec, row_spec), check_vma=False)
```

time: 424 us -> 388 us (0.915)
  Pallas kernels: 0 us -> 371 us
  waiting for transfers between devices: 303 us -> 0.01 us
  local copies, waits for them, and re-layouts: 37.4 us -> 5.69 us
  matrix products: 32.7 us -> 1.96 us
  starting transfers between devices: 24.7 us -> 5.66 us
  between operations: 14.3 us -> 0.7 us
  other arithmetic: 11.6 us -> 2.13 us
    pallas_call x0 -> x5, Pallas kernels: none -> 371 us  [the longest x1 213 us: local_backward(): pl.pallas_call(functools.partial(gather_kernel, fs_n), out_shape=jax.Shap...]
    all_gather x2 -> x0, waiting for transfers between devices: 180 us -> none  [the longest x1 180 us: local_backward(): dh_all = lax.all_gather(jnp.stack([dh_gate, dh_up]), 'fsdp', axis=0)]
    all_to_all x5 -> x0, waiting for transfers between devices: 123 us -> none  [the longest x1 92.9 us: local_backward(): h_all = lax.all_to_all(h_both, 'fsdp', 0, 0, tiled=True)]
    dot_general x6 -> x2, matrix products: 32.7 us -> 1.96 us  [the longest x1 0.99 us: local_backward(): jnp.dot(pick, grad_out, preferred_element_type=F32).astype(BF16)]
    all_to_all x5 -> x0, starting transfers between devices: 21.7 us -> none  [the longest x1 5.23 us: local_backward(): lax.all_to_all(send_gate, 'ep', 0, 0, tiled=True)]
    reshape x6 -> x0, local copies, waits for them, and re-layouts: 10.8 us -> none  [the longest x1 5.18 us: local_backward(): jnp.einsum('erd,serf->edsf', x_rows, dh_g, preferred_element_type=f32)]
    slice x1 -> x0, local copies, waits for them, and re-layouts: 5.55 us -> none  [local_backward(): dh_g = dh_all[:, 0]]
    gather x4 -> x0, local copies, waits for them, and re-layouts: 5.22 us -> none  [the longest x1 1.89 us: local_backward(): jnp.take(gates.reshape(-1), src_choice, mode='fill', fill_value=0)]
  transfers between devices with their start and end apart: 8 -> 1, of which waited for: 5 -> 0; matrix products, arithmetic and copies ran while one was open for 11% -> 0% of each run, Pallas kernels for 0% -> 5%
where the time goes in v2:
time: 388 us; the launch traced here: 387 us
  Pallas kernels  371 us (96%)
  local copies, waits for them, and re-layouts  5.69 us (1%)
  starting transfers between devices  5.66 us (1%)
    pallas_call x1, Pallas kernels, local_backward(): pl.pallas_call(functools.partial(gather_kernel, fs_n), out_shape=jax.Shap...  213 us
    pallas_call x1, Pallas kernels, local_backward(): pl.pallas_call(functools.partial(exchange_kernel, fs_n, ep_n), out_shape=...  114 us
    pallas_call x1, Pallas kernels, local_backward(): pl.pallas_call(dw_kernel, grid=(e_loc, fs_n), out_shape=(jax.ShapeDtypeSt...  20 us
    pallas_call x1, Pallas kernels, local_backward(): pl.pallas_call(dx_kernel, grid=(e_loc, fs_n), out_shape=jax.ShapeDtypeStr...  15.9 us
  transfers between devices with their start and end apart: 1, of which 0 were waited for; matrix products, arithmetic and copies ran while one was open for 0% of the time, Pallas kernels for 5%

profile of v2, /device:TPU:0, one launch (start us, length us, event | category | flops | bytes accessed | tf_op | source)
XLA Modules:
  0.0 386.8 jit_solution(10881227941397914631)
XLA Ops:
  0.6 0.0 copy-start
  0.6 0.7 fusion.4
  1.4 0.2 copy-done
  1.6 1.0 convolution_convert_fusion
  2.6 0.8 select_reduce_fusion.1
  3.4 0.1 broadcast_in_dim.41
  3.5 1.5 reshape.220
  5.0 0.9 copy.27
  5.9 0.8 broadcast_in_dim.42.gt_s
  6.6 114.4 %exchange.1 = (bf16[2,4,4,64,768]{4,3,2,1,0:T(8,128)(2,1)}, bf16[4,4,64,192]{3,2,1,0:T(8,128)(2,1)}, bf16[4,4,8,8,768]{4,3,2,1,0:T(8,128)(2,1)}, f32[8,4,8,128]{3,2,1,0:T(8,128)}) custom-call(bf16[4,64,3072]{2,1,0:T(8,128)(2,1)} %hg.1, bf16[4,64,3072]{2,1,0:T(8,128)(2,1)} %hu.1, bf16[4,4,64,192]{3,2,1,0:T(8,128)(2,1)} %bitcast.30, ...), custom_call_target="tpu_custom_call" | custom-call | tf_op jit(solution)/shard_map/exchange/pallas_call | solution.py:199
  121.1 7.3 %hidden.1 = (bf16[2,4,256,768]{3,2,1,0:T(8,128)(2,1)}, bf16[4,256,768]{2,1,0:T(8,128)(2,1)}) custom-call(bf16[4,256,768]{2,1,0:T(8,128)(2,1)} %bitcast.32, bf16[2,4,256,768]{3,2,1,0:T(8,128)(2,1)} %bitcast.29, bf16[4,768,768]{2,1,0:T(8,128)(2,1)} %w.1), custom_call_target="tpu_custom_call" | custom-call | tf_op jit(solution)/shard_map/hidden/pallas_call | solution.py:225
  128.4 213.0 %gather.1.dh = bf16[4,2,4,256,768]{4,3,2,1,0:T(8,128)(2,1)} custom-call(bf16[2,4,256,768]{3,2,1,0:T(8,128)(2,1)} %get-tuple-element.16.dh), custom_call_target="tpu_custom_call" | custom-call | tf_op jit(solution)/shard_map/gather/pallas_call | solution.py:240
  341.4 0.0 copy-start.2
  341.4 15.9 %dx.1 = bf16[4,256,192]{2,1,0:T(8,128)(2,1)} custom-call(bf16[4,2,4,256,768]{4,3,2,1,0:T(8,128)(2,1)} %gather.1.dh, bf16[4,192,3072]{2,1,0:T(8,128)(2,1)} %wg.1, bf16[4,192,3072]{2,1,0:T(8,128)(2,1)} %wu.1), custom_call_target="tpu_custom_call" | custom-call | tf_op jit(solution)/shard_map/dx/pallas_call | solution.py:251
  357.3 1.9 copy_bitcast_fusion
  359.2 5.7 %all-to-all-start = ((bf16[32,4,8,192]{3,2,1,0:T(8,128)(2,1)}), bf16[32,4,8,192]{3,2,1,0:T(8,128)(2,1)S(1)}, u32[]{:S(2)}, u32[]{:S(2)}) async-start(bf16[32,4,8,192]{3,2,1,0:T(8,128)(2,1)} %copy_bitcast_fusion), calls=%async_computation | async-start | bytes 1048576 | tf_op jit(solution)/shard_map/all_to_all | solution.py:261
  364.9 0.0 copy-done.2
  364.9 0.1 copy.24
  364.9 0.6 select_reduce_fusion
  365.6 0.0 copy-start.1
  365.6 20.0 %dw.1 = (f32[4,192,3072]{2,1,0:T(8,128)}, f32[4,192,3072]{2,1,0:T(8,128)}, f32[4,768,768]{2,1,0:T(8,128)}) custom-call(bf16[4,256,192]{2,1,0:T(8,128)(2,1)} %bitcast.41, bf16[4,2,4,256,768]{4,3,2,1,0:T(8,128)(2,1)} %gather.1.dh, bf16[4,256,768]{2,1,0:T(8,128)(2,1)} %get-tuple-element.19.act, bf16[4,256,768]{2,1,0:T(8,128)(2,1)} %bitcast.33), custom_call_target="tpu_custom_call" | custom-call | flops 4831838208 | bytes 50000000 | tf_op jit(solution)/shard_map/dw/pallas_call | solution.py:264
  385.6 0.0 all-to-all-done
  385.6 0.2 copy.22
  385.8 1.0 convolution_convert_fusion.1
  386.8 0.0 copy-done.1
Async XLA Ops:
  0.6 1.0 copy-start
  341.4 23.5 %copy-start.2 = (f32[8,4,8,128]{3,2,1,0:T(8,128)S(1)}, f32[8,4,8,128]{3,2,1,0:T(8,128)}, u32[]{:S(2)}) copy-start(f32[8,4,8,128]{3,2,1,0:T(8,128)} %get-tuple-element.17) | copy-start | bytes 393220
  359.2 26.4 %all-to-all-start = ((bf16[32,4,8,192]{3,2,1,0:T(8,128)(2,1)}), bf16[32,4,8,192]{3,2,1,0:T(8,128)(2,1)S(1)}, u32[]{:S(2)}, u32[]{:S(2)}) async-start(bf16[32,4,8,192]{3,2,1,0:T(8,128)(2,1)} %copy_bitcast_fusion), calls=%async_computation | async-start | bytes 1048576 | tf_op jit(solution)/shard_map/all_to_all | solution.py:261
  365.6 21.2 %copy-start.1 = (bf16[128,768]{1,0:T(8,128)(2,1)S(1)}, bf16[128,768]{1,0:T(8,128)(2,1)}, u32[]{:S(2)}) copy-start(bf16[128,768]{1,0:T(8,128)(2,1)} %param.11) | copy-start | bytes 589828
